TPU v7x, 512 devices: a whole 4x4x16 slice. The times are simulated.
512 devices in a mesh: dp: 32 (over y, z_hi, core), tensor: 16 (over z_lo, x).
Axes of the slice: x: 4, y: 4, z: 16 (z_hi: 4, z_lo: 4; z = z_hi * 4 + z_lo), core: 2. Of those that a mesh axis runs over, the one named last changes fastest.
Arguments:
- acts: bfloat16 [12288, 4096], P('dp', 'tensor'), may hold values from -6 to 6
- grad_out: bfloat16 [12288, 4096], P('dp', 'tensor'), may hold values from -60 to 60
- gate_pre: bfloat16 [12288, 14336], P('dp', 'tensor'), may hold values from -6 to 6
- up_pre: bfloat16 [12288, 14336], P('dp', 'tensor'), may hold values from -6 to 6
- down_weight: bfloat16 [14336, 4096], P('tensor', 'dp'), may hold values from -0.09375 to 0.09375
- proj_in: bfloat16 [4096, 64], P('tensor'), may hold values from -0.09375 to 0.09375
- proj_out: bfloat16 [14336, 64], P('tensor'), may hold values from -0.046875 to 0.046875
- lengths: int32 [96], P('dp'), may hold values from 64 to 128
- query_ids: int32 [16], replicated, may hold values from 0 to 95
Outputs:
- gram: float32 [4096, 4096], P('dp', 'tensor')
- scores: float32 [16, 96], P(None, 'dp')
Inputs may be any that keep to these rules, and one draw needn't show every extreme that they name: `query_ids`: queries may repeat.
All inputs are finite; a program needn't handle non-finite values.
Results may differ from a plain program's by a relative error of at most 0.004.
Values may be sent and summed in bfloat16 or wider, within the bound.
No kernel may reach another device: no remote copies, remote signals or barrier semaphores. Data moves between devices by JAX's collectives and lax.ppermute only.
A program may use at most 64 MiB of HBM per device.

v0:
```python
import jax
import jax.numpy as jnp
from jax import lax
from jax.sharding import Mesh
from jax.sharding import PartitionSpec as P

TENSOR = ("tensor_0", "tensor_1")


def in_order(parts, dim):
    shape = list(parts.shape[1:])
    shape[dim] *= parts.shape[0]
    return jnp.moveaxis(parts, 0, dim).reshape(shape)


def stacked_from(array, axes, order):
    parts = array
    for k in order:
        parts = lax.all_gather(parts, axes[k])
    done = order[::-1]
    back = [done.index(k) for k in range(len(axes))]
    parts = parts.transpose(*back, *range(len(axes), parts.ndim))
    return parts.reshape(-1, *array.shape)


def whole_of(array, axes, order, dim):
    return in_order(stacked_from(array, axes, order), dim)


def filled_up(lines, count):
    spare = -len(lines) % count
    return jnp.pad(lines, [(0, spare)] + [(0, 0)] * (lines.ndim - 1))


def from_everyone(array, axis):
    count = lax.axis_size(axis)
    return lax.all_to_all(
        jnp.broadcast_to(array[None], (count, *array.shape)), axis, 0, 0, tiled=True
    )


def gather_directly(array, axis, dim):
    return in_order(from_everyone(array, axis), dim)


def split_up(array, dim, count):
    shape = array.shape
    parts = array.reshape(*shape[:dim], count, shape[dim] // count, *shape[dim + 1 :])
    return jnp.moveaxis(parts, dim, 0)


def sum_at_owner(array, axis, dim):
    count = lax.axis_size(axis)
    parts = lax.all_to_all(split_up(array, dim, count), axis, 0, 0, tiled=True)
    return jnp.sum(parts, axis=0)


def sum_by_parts(array, axes):
    padded = filled_up(array, lax.axis_size(axes))
    whole = gather_directly(sum_at_owner(padded, axes, 0), axes, 0)
    return lax.slice_in_dim(whole, 0, len(array)).reshape(array.shape)


def together(arrays, axis):
    flat, at, gathered = (jnp.concatenate([a.reshape(-1) for a in arrays]), 0, [])
    subtotal = sum_by_parts(flat, axis)
    for a in arrays:
        gathered.append(subtotal[at : at + a.size].reshape(a.shape))
        at += a.size
    return tuple(gathered)


def silu_slope(value):
    sigma = jax.nn.sigmoid(value)
    return sigma + value * sigma * (1.0 - sigma)


def body(acts, grad_out, gate_pre, up_pre, down_weight, proj_in, proj_out, lengths, query_ids):
    highest = lax.Precision.HIGHEST
    tokens_here = acts.shape[0]
    examples_here = lengths.shape[0]
    seq_len = tokens_here // examples_here
    full_grad = whole_of(grad_out, TENSOR, (0, 1), 1)
    hidden_grad = lax.dot_general(
        full_grad,
        lax.all_gather(down_weight, "dp", axis=1, tiled=True),
        (((1,), (1,)), ((), ())),
        preferred_element_type=jnp.float32,
    )
    gate_value = gate_pre.astype(jnp.float32)
    gate_grad = (hidden_grad * up_pre.astype(jnp.float32) * silu_slope(gate_value)).astype(
        jnp.bfloat16
    )
    out_part = jnp.dot(gate_grad, proj_out, preferred_element_type=jnp.float32)
    in_part = jnp.dot(acts, proj_in, preferred_element_type=jnp.float32)
    out_factor, in_factor = together((out_part, in_part), TENSOR)
    positions = lax.broadcasted_iota(jnp.int32, (examples_here, seq_len), 1)
    live = (positions < lengths[:, None]).astype(jnp.float32)
    out_factor = out_factor.reshape(examples_here, seq_len, -1) * live[:, :, None]
    in_factor = in_factor.reshape(examples_here, seq_len, -1)
    features = jnp.einsum("esa,esb->eab", out_factor, in_factor, precision=highest).reshape(
        examples_here, -1
    )
    width = features.shape[1]
    first_example = lax.axis_index("dp") * examples_here
    example_ids = first_example + lax.broadcasted_iota(jnp.int32, (1, examples_here), 1)
    selector = (query_ids[:, None] == example_ids).astype(jnp.float32)
    query_part = jnp.dot(selector, features, precision=highest)
    local_square = jnp.sum(features * features)
    query_feat, total_square = together((query_part, local_square), "dp")
    examples_all = examples_here * lax.axis_size("dp")
    norm_mean = total_square / examples_all + 1e-06
    col_width = width // lax.axis_size(TENSOR)
    own_cols = lax.dynamic_slice_in_dim(features, lax.axis_index(TENSOR) * col_width, col_width, 1)
    row_block = lax.all_to_all(features, "dp", split_axis=1, concat_axis=0, tiled=True)
    block = lax.dot_general(
        row_block,
        gather_directly(own_cols, "dp", 0),
        (((0,), (0,)), ((), ())),
        precision=highest,
        preferred_element_type=jnp.float32,
    )
    gram = block * (width / examples_all) / norm_mean
    scores = jnp.dot(query_feat, features.T, precision=highest) / norm_mean
    return (gram, scores)


def solution(mesh):
    split = Mesh(mesh.devices.reshape(mesh.shape["dp"], 4, 4), ("dp", "tensor_0", "tensor_1"))
    in_specs = (
        P("dp", TENSOR),
        P("dp", TENSOR),
        P("dp", TENSOR),
        P("dp", TENSOR),
        P(TENSOR, "dp"),
        P(TENSOR, None),
        P(TENSOR, None),
        P("dp"),
        P(),
    )
    out_specs = (P("dp", TENSOR), P(None, "dp"))
    return jax.shard_map(body, mesh=split, in_specs=in_specs, out_specs=out_specs, check_vma=False)
```

profile of v0, /device:TPU:1, one launch (start us, length us, event | category | flops | bytes accessed | tf_op | source)
XLA Modules:
  0.0 366.1 jit_solution(10889218226166880357)
XLA Ops:
  7.2 20.1 %all-gather = bf16[1536,256]{1,0:T(8,128)(2,1)} all-gather(bf16[384,256]{1,0:T(8,128)(2,1)} %param.10), channel_id=2, replica_groups=mesh['dp'=32,'tensor_0'=4,'tensor_1'=4] {'tensor_0'}, dimensions={0}, use_global_device_ids=true | all-gather | bytes 983040 | tf_op jit(solution)/shard_map/all_gather | solution.py:19
  27.4 0.7 all-gather.5.cloned.1.call-update
  28.4 50.3 %all-gather.7.cloned.1.call-done = bf16[16,384,256]{2,1,0:T(8,128)(2,1)} async-done(((bf16[4,384,256]{2,1,0:T(8,128)(2,1)}), bf16[16,384,256]{2,1,0:T(8,128)(2,1)}) %all-gather.7.cloned.1.call-update) | async-done | bytes 3145744 | tf_op jit(solution)/shard_map/all_gather | solution.py:19
  78.7 2.1 copy.42
  80.8 2.8 copy.43
  83.6 132.9 %all-gather.5.cloned.1.call-done = bf16[896,4096]{1,0:T(8,128)(2,1)} async-done(((bf16[896,128]{1,0:T(8,128)(2,1)}), bf16[896,4096]{1,0:T(8,128)(2,1)}) %all-gather.5.cloned.1.call-update) | async-done | bytes 7340048 | tf_op jit(solution)/shard_map/all_gather | solution.py:86
  216.5 8.0 %fusion.7 = f32[384,64]{1,0:T(8,128)S(1)} fusion(bf16[896,64]{0,1:T(8,128)(2,1)} %param.15, bf16[384,896]{1,0:T(8,128)(2,1)} %param.11, bf16[384,896]{1,0:T(8,128)(2,1)} %param.12, bf16[384,4096]{0,1:T(8,128)(2,1)} %bitcast.35, bf16[896,4096]{1,0:T(8,128)(2,1)} %all-gather.5.cloned.1.call-done), kind=kOutput, calls=%fused_computation.11 | convolution fusion | flops 2866741248 | bytes 12075008 | tf_op jit(solution)/shard_map/dot_general | solution.py:94
  224.6 0.2 copy.46
  224.8 12.5 %all_to_all.51 = f32[16,1,3072]{2,1,0:T(1,128)S(1)} all-to-all(f32[16,1,3072]{2,1,0:T(1,128)S(1)} %copy.46), channel_id=1, replica_groups=mesh['dp'=32,'tensor_0'=4,'tensor_1'=4] {'tensor_0','tensor_1'}, dimensions={0} | all-to-all | bytes 393216 | tf_op jit(solution)/shard_map/all_to_all | solution.py:54
  237.4 0.8 broadcast_in_dim.6
  238.2 3.9 %all-to-all-start.1 = ((f32[16,1,3072]{2,1,0:T(1,128)}), f32[16,1,3072]{2,1,0:T(1,128)S(1)}, u32[]{:S(2)}, u32[]{:S(2)}) async-start(f32[16,1,3072]{2,1,0:T(1,128)} %broadcast_in_dim.6), calls=%async_computation.1 | async-start | bytes 393216 | tf_op jit(solution)/shard_map/all_to_all | solution.py:37
  242.2 8.2 %all-to-all-done.1 = f32[16,1,3072]{2,1,0:T(1,128)S(1)} async-done(((f32[16,1,3072]{2,1,0:T(1,128)}), f32[16,1,3072]{2,1,0:T(1,128)S(1)}, u32[]{:S(2)}, u32[]{:S(2)}) %all-to-all-start.1) | async-done | bytes 196640 | tf_op jit(solution)/shard_map/all_to_all | solution.py:37
  250.4 0.5 slice_reduce_fusion.1
  251.1 1.2 multiply_reduce_fusion
  252.4 0.3 convolution_bitcast_fusion
  252.8 0.7 select_maximum_fusion
  253.4 1.1 all_to_all.42
  254.5 11.2 %all-to-all-start.4 = ((f32[32,1,2049]{2,1,0:T(1,128)}), f32[32,1,2049]{2,1,0:T(1,128)S(1)}, u32[]{:S(2)}, u32[]{:S(2)}) async-start(f32[32,1,2049]{2,1,0:T(1,128)} %all_to_all.42), calls=%async_computation.4 | async-start | bytes 557056 | tf_op jit(solution)/shard_map/all_to_all | solution.py:54
  265.8 0.7 copy.49
  266.5 19.6 %all-to-all-done.4 = f32[32,1,2049]{2,1,0:T(1,128)S(1)} async-done(((f32[32,1,2049]{2,1,0:T(1,128)}), f32[32,1,2049]{2,1,0:T(1,128)S(1)}, u32[]{:S(2)}, u32[]{:S(2)}) %all-to-all-start.4) | async-done | bytes 262304 | tf_op jit(solution)/shard_map/all_to_all | solution.py:54
  286.1 7.2 %all-to-all-start.2 = ((f32[3,32,128]{2,0,1:T(4,128)}), f32[3,32,128]{2,0,1:T(4,128)S(1)}, u32[]{:S(2)}, u32[]{:S(2)}) async-start(f32[3,32,128]{2,0,1:T(4,128)} %copy.49), calls=%async_computation.2 | async-start | bytes 131072 | tf_op jit(solution)/shard_map/all_to_all | solution.py:115
  293.4 14.8 %all-to-all-done.2 = f32[3,32,128]{2,0,1:T(4,128)S(1)} async-done(((f32[3,32,128]{2,0,1:T(4,128)}), f32[3,32,128]{2,0,1:T(4,128)S(1)}, u32[]{:S(2)}, u32[]{:S(2)}) %all-to-all-start.2) | async-done | bytes 49184 | tf_op jit(solution)/shard_map/all_to_all | solution.py:115
  308.2 0.9 broadcast_in_dim.8
  309.1 3.8 %all-to-all-start.5 = ((f32[32,1,2049]{2,1,0:T(1,128)}), f32[32,1,2049]{2,1,0:T(1,128)S(1)}, u32[]{:S(2)}, u32[]{:S(2)}) async-start(f32[32,1,2049]{2,1,0:T(1,128)} %broadcast_in_dim.8), calls=%async_computation.5 | async-start | bytes 557056 | tf_op jit(solution)/shard_map/all_to_all | solution.py:37
  312.9 17.7 %all-to-all-done.5 = f32[32,1,2049]{2,1,0:T(1,128)S(1)} async-done(((f32[32,1,2049]{2,1,0:T(1,128)}), f32[32,1,2049]{2,1,0:T(1,128)S(1)}, u32[]{:S(2)}, u32[]{:S(2)}) %all-to-all-start.5) | async-done | bytes 262304 | tf_op jit(solution)/shard_map/all_to_all | solution.py:37
  330.6 0.7 broadcast_in_dim.7
  331.3 9.4 %all-to-all-start.3 = ((f32[32,3,256]{2,1,0:T(4,128)}), f32[32,3,256]{2,1,0:T(4,128)S(1)}, u32[]{:S(2)}, u32[]{:S(2)}) async-start(f32[32,3,256]{2,1,0:T(4,128)} %broadcast_in_dim.7), calls=%async_computation.3 | async-start | bytes 262144 | tf_op jit(solution)/shard_map/all_to_all | solution.py:37
  340.7 0.7 reduce.5
  341.5 0.5 slice.25
  342.8 1.0 convolution_divide_fusion
  343.8 14.5 %all-to-all-done.3 = f32[32,3,256]{2,1,0:T(4,128)S(1)} async-done(((f32[32,3,256]{2,1,0:T(4,128)}), f32[32,3,256]{2,1,0:T(4,128)S(1)}, u32[]{:S(2)}, u32[]{:S(2)}) %all-to-all-start.3) | async-done | bytes 98336 | tf_op jit(solution)/shard_map/all_to_all | solution.py:37
  358.3 1.0 fusion.9
  (28 shorter events, 1.6 us)
Async XLA Ops:
  7.2 20.9 %copy-start = (bf16[384,256]{1,0:T(8,128)(2,1)S(1)}, bf16[384,256]{1,0:T(8,128)(2,1)}, u32[]{:S(2)}) copy-start(bf16[384,256]{1,0:T(8,128)(2,1)} %param.9) | copy-start | bytes 589828
  7.2 20.9 %copy-start.1 = (bf16[256,64]{0,1:T(8,128)(2,1)S(1)}, bf16[256,64]{0,1:T(8,128)(2,1)}, u32[]{:S(2)}) copy-start(bf16[256,64]{0,1:T(8,128)(2,1)} %param.14) | copy-start | bytes 98308
  7.2 71.5 %all-gather.7.cloned.1.call-start = ((), (), s32[]{:S(2)}) async-start(), calls=%async_computation.7 | async-start | bytes 3932160 | tf_op jit(solution)/shard_map/all_gather | solution.py:19
  27.3 189.2 %all-gather.5.cloned.1.call-start = ((), (), s32[]{:S(2)}) async-start(), calls=%async_computation.6 | async-start | bytes 7569408 | tf_op jit(solution)/shard_map/all_gather | solution.py:86
  224.5 17.7 %copy-start.3 = (s32[3]{0:T(128)S(1)}, s32[3]{0:T(128)}, u32[]{:S(2)}) copy-start(s32[3]{0:T(128)} %param.16) | copy-start | bytes 40
  224.8 27.6 %copy-start.2 = (s32[16]{0:T(128)S(1)}, s32[16]{0:T(128)}, u32[]{:S(2)}) copy-start(s32[16]{0:T(128)} %param.17) | copy-start | bytes 196
  238.2 12.2 %all-to-all-start.1 = ((f32[16,1,3072]{2,1,0:T(1,128)}), f32[16,1,3072]{2,1,0:T(1,128)S(1)}, u32[]{:S(2)}, u32[]{:S(2)}) async-start(f32[16,1,3072]{2,1,0:T(1,128)} %broadcast_in_dim.6), calls=%async_computation.1 | async-start | bytes 393216 | tf_op jit(solution)/shard_map/all_to_all | solution.py:37
  254.5 31.5 %all-to-all-start.4 = ((f32[32,1,2049]{2,1,0:T(1,128)}), f32[32,1,2049]{2,1,0:T(1,128)S(1)}, u32[]{:S(2)}, u32[]{:S(2)}) async-start(f32[32,1,2049]{2,1,0:T(1,128)} %all_to_all.42), calls=%async_computation.4 | async-start | bytes 557056 | tf_op jit(solution)/shard_map/all_to_all | solution.py:54
  286.1 22.1 %all-to-all-start.2 = ((f32[3,32,128]{2,0,1:T(4,128)}), f32[3,32,128]{2,0,1:T(4,128)S(1)}, u32[]{:S(2)}, u32[]{:S(2)}) async-start(f32[3,32,128]{2,0,1:T(4,128)} %copy.49), calls=%async_computation.2 | async-start | bytes 131072 | tf_op jit(solution)/shard_map/all_to_all | solution.py:115
  309.1 21.5 %all-to-all-start.5 = ((f32[32,1,2049]{2,1,0:T(1,128)}), f32[32,1,2049]{2,1,0:T(1,128)S(1)}, u32[]{:S(2)}, u32[]{:S(2)}) async-start(f32[32,1,2049]{2,1,0:T(1,128)} %broadcast_in_dim.8), calls=%async_computation.5 | async-start | bytes 557056 | tf_op jit(solution)/shard_map/all_to_all | solution.py:37
  331.3 27.0 %all-to-all-start.3 = ((f32[32,3,256]{2,1,0:T(4,128)}), f32[32,3,256]{2,1,0:T(4,128)S(1)}, u32[]{:S(2)}, u32[]{:S(2)}) async-start(f32[32,3,256]{2,1,0:T(4,128)} %broadcast_in_dim.7), calls=%async_computation.3 | async-start | bytes 262144 | tf_op jit(solution)/shard_map/all_to_all | solution.py:37
Sparse Core Ops, SparseCore 0:
  27.4 51.1 all-gather.6
  81.7 134.7 all-gather.4
where the time goes:
time: 367 us; the launch traced here: 366 us
  waiting for transfers between devices  259 us (71%)
  starting transfers between devices  35.5 us (10%)
  blocking collectives  32.5 us (9%)
  between operations  14.9 us (4%)
  matrix products  11.6 us (3%)
  local copies, waits for them, and re-layouts  11.1 us (3%)
    all_gather x1, waiting for transfers between devices, body(): lax.all_gather(down_weight, 'dp', axis=1, tiled=True)  133 us
    all_gather x1, waiting for transfers between devices, stacked_from(): parts = lax.all_gather(parts, axes[k])  50.3 us
    all_to_all x3, waiting for transfers between devices, from_everyone(): lax.all_to_all(jnp.broadcast_to(array[None], (count, *array.shape)), axis...  40.4 us
    all_gather x1, blocking collectives, stacked_from(): parts = lax.all_gather(parts, axes[k])  20.1 us
    all_to_all x1, waiting for transfers between devices, sum_at_owner(): parts = lax.all_to_all(split_up(array, dim, count), axis, 0, 0, tiled=True)  19.6 us
    all_to_all x3, starting transfers between devices, from_everyone(): lax.all_to_all(jnp.broadcast_to(array[None], (count, *array.shape)), axis...  17.1 us
    all_to_all x1, waiting for transfers between devices, body(): lax.all_to_all(features, 'dp', split_axis=1, concat_axis=0, tiled=True)  14.8 us
    all_to_all x1, blocking collectives, sum_at_owner(): parts = lax.all_to_all(split_up(array, dim, count), axis, 0, 0, tiled=True)  12.5 us
  transfers between devices with their start and end apart: 7, of which 7 were waited for; matrix products, arithmetic and copies ran while one was open for 2% of the time, Pallas kernels for 0%

commit v1 on v0

--- a/solution.py
+++ b/solution.py
@@ -76,6 +76,12 @@
 
 
 def body(acts, grad_out, gate_pre, up_pre, down_weight, proj_in, proj_out, lengths, query_ids):
+
+    def mix_the_frame(base_x):
+        return jnp.concatenate(
+            lax.all_to_all(jnp.stack(lax.axis_size("dp") * [base_x]), "dp", 0, 0), 1
+        )
+
     highest = lax.Precision.HIGHEST
     tokens_here = acts.shape[0]
     examples_here = lengths.shape[0]
@@ -83,7 +89,7 @@
     full_grad = whole_of(grad_out, TENSOR, (0, 1), 1)
     hidden_grad = lax.dot_general(
         full_grad,
-        lax.all_gather(down_weight, "dp", axis=1, tiled=True),
+        mix_the_frame(down_weight),
         (((1,), (1,)), ((), ())),
         preferred_element_type=jnp.float32,
     )

time: 367 us -> 570 us (1.55)
  blocking collectives: 32.5 us -> 345 us
  waiting for transfers between devices: 259 us -> 121 us
  starting transfers between devices: 35.5 us -> 58.2 us
    all_gather x1, blocking collectives: 20.1 us -> 331 us  [stacked_from(): parts = lax.all_gather(parts, axes[k])]
    all_gather x1 -> x0, waiting for transfers between devices: 133 us -> none  [body(): lax.all_gather(down_weight, 'dp', axis=1, tiled=True)]
    all_to_all x0 -> x1, starting transfers between devices: none -> 19.5 us  [mix_the_frame(): lax.all_to_all(jnp.stack(lax.axis_size('dp') * [base_x]), 'dp', 0, 0)]
  transfers between devices with their start and end apart: 7 -> 7, of which waited for: 7 -> 6; matrix products, arithmetic and copies ran while one was open for 2% -> 1% of each run, Pallas kernels for 0% -> 0%
where the time goes in v1:
time: 570 us
  blocking collectives  345 us (61%)
  waiting for transfers between devices  121 us (21%)
  starting transfers between devices  58.2 us (10%)
  local copies, waits for them, and re-layouts  16.3 us (3%)
  between operations  14.9 us (3%)
  matrix products  11.8 us (2%)
    all_gather x1, blocking collectives, stacked_from(): parts = lax.all_gather(parts, axes[k])  331 us
    all_gather x1, waiting for transfers between devices, stacked_from(): parts = lax.all_gather(parts, axes[k])  46.4 us
    all_to_all x3, waiting for transfers between devices, from_everyone(): lax.all_to_all(jnp.broadcast_to(array[None], (count, *array.shape)), axis...  40.4 us
    all_to_all x1, waiting for transfers between devices, sum_at_owner(): parts = lax.all_to_all(split_up(array, dim, count), axis, 0, 0, tiled=True)  19.6 us
    all_to_all x1, starting transfers between devices, mix_the_frame(): lax.all_to_all(jnp.stack(lax.axis_size('dp') * [base_x]), 'dp', 0, 0)  19.5 us
    all_to_all x3, starting transfers between devices, from_everyone(): lax.all_to_all(jnp.broadcast_to(array[None], (count, *array.shape)), axis...  17.1 us
    all_to_all x1, waiting for transfers between devices, body(): lax.all_to_all(features, 'dp', split_axis=1, concat_axis=0, tiled=True)  14.9 us
    all_to_all x1, starting transfers between devices, sum_at_owner(): parts = lax.all_to_all(split_up(array, dim, count), axis, 0, 0, tiled=True)  14.9 us
  transfers between devices with their start and end apart: 7, of which 6 were waited for; matrix products, arithmetic and copies ran while one was open for 1% of the time, Pallas kernels for 0%

profile of v1, /device:TPU:1, one launch (start us, length us, event | category | flops | bytes accessed | tf_op | source)
XLA Modules:
  0.0 569.5 jit_solution(13671894004950990890)
XLA Ops:
  7.2 1.1 copy.48
  8.3 4.1 stack.2
  12.4 19.5 %all-to-all-start = ((bf16[32,896,128]{1,2,0:T(8,128)(2,1)}), bf16[32,896,128]{1,2,0:T(8,128)(2,1)}, u32[]{:S(2)}, u32[]{:S(2)}) async-start(bf16[32,896,128]{1,2,0:T(8,128)(2,1)} %stack.2), calls=%async_computation | async-start | bytes 14680064 | tf_op jit(solution)/shard_map/all_to_all | solution.py:82
  32.0 331.1 %all-gather = bf16[1536,256]{1,0:T(8,128)(2,1)} all-gather(bf16[384,256]{1,0:T(8,128)(2,1)S(1)} %copy-done.1), channel_id=2, replica_groups=mesh['dp'=32,'tensor_0'=4,'tensor_1'=4] {'tensor_0'}, dimensions={0}, use_global_device_ids=true | all-gather | bytes 983040 | tf_op jit(solution)/shard_map/all_gather | solution.py:19
  363.5 46.4 %all-gather.4.cloned.1.call-done = bf16[16,384,256]{2,1,0:T(8,128)(2,1)} async-done(((bf16[4,384,256]{2,1,0:T(8,128)(2,1)}), bf16[16,384,256]{2,1,0:T(8,128)(2,1)}) %all-gather.4.cloned.1.call-update) | async-done | bytes 3145744 | tf_op jit(solution)/shard_map/all_gather | solution.py:19
  409.9 2.1 copy.46
  412.0 2.8 copy.47
  414.8 8.2 %fusion.7 = f32[384,64]{1,0:T(8,128)S(1)} fusion(bf16[896,64]{0,1:T(8,128)(2,1)} %param.15, bf16[384,896]{1,0:T(8,128)(2,1)} %param.11, bf16[384,896]{1,0:T(8,128)(2,1)} %param.12, bf16[384,4096]{0,1:T(8,128)(2,1)} %bitcast.38, bf16[896,4096]{0,1:T(8,128)(2,1)} %bitcast.7), kind=kOutput, calls=%fused_computation.11 | convolution fusion | flops 2866741248 | bytes 12075008 | tf_op jit(solution)/shard_map/dot_general | solution.py:100
  423.4 14.1 %all_to_all.56 = f32[16,1,3072]{2,1,0:T(1,128)S(1)} all-to-all(f32[16,1,3072]{2,1,0:T(1,128)S(1)} %copy.51), channel_id=1, replica_groups=mesh['dp'=32,'tensor_0'=4,'tensor_1'=4] {'tensor_0','tensor_1'}, dimensions={0} | all-to-all | bytes 393216 | tf_op jit(solution)/shard_map/all_to_all | solution.py:54
  437.6 0.8 broadcast_in_dim.6
  438.4 4.1 all-to-all-start.2
  442.6 8.2 %all-to-all-done.2 = f32[16,1,3072]{2,1,0:T(1,128)S(1)} async-done(((f32[16,1,3072]{2,1,0:T(1,128)}), f32[16,1,3072]{2,1,0:T(1,128)S(1)}, u32[]{:S(2)}, u32[]{:S(2)}) %all-to-all-start.2) | async-done | bytes 196640 | tf_op jit(solution)/shard_map/all_to_all | solution.py:37
  450.8 0.5 slice_reduce_fusion.1
  451.5 1.2 multiply_reduce_fusion
  452.8 0.3 convolution_bitcast_fusion
  453.1 0.7 select_maximum_fusion
  453.8 1.1 all_to_all.46
  454.9 14.9 %all-to-all-start.5 = ((f32[32,1,2049]{2,1,0:T(1,128)}), f32[32,1,2049]{2,1,0:T(1,128)S(1)}, u32[]{:S(2)}, u32[]{:S(2)}) async-start(f32[32,1,2049]{2,1,0:T(1,128)} %all_to_all.46), calls=%async_computation.5 | async-start | bytes 557056 | tf_op jit(solution)/shard_map/all_to_all | solution.py:54
  469.9 0.7 copy.54
  470.5 19.6 %all-to-all-done.5 = f32[32,1,2049]{2,1,0:T(1,128)S(1)} async-done(((f32[32,1,2049]{2,1,0:T(1,128)}), f32[32,1,2049]{2,1,0:T(1,128)S(1)}, u32[]{:S(2)}, u32[]{:S(2)}) %all-to-all-start.5) | async-done | bytes 262304 | tf_op jit(solution)/shard_map/all_to_all | solution.py:54
  490.1 6.6 %all-to-all-start.3 = ((f32[3,32,128]{2,0,1:T(4,128)}), f32[3,32,128]{2,0,1:T(4,128)S(1)}, u32[]{:S(2)}, u32[]{:S(2)}) async-start(f32[3,32,128]{2,0,1:T(4,128)} %copy.54), calls=%async_computation.3 | async-start | bytes 131072 | tf_op jit(solution)/shard_map/all_to_all | solution.py:121
  496.9 14.9 %all-to-all-done.3 = f32[3,32,128]{2,0,1:T(4,128)S(1)} async-done(((f32[3,32,128]{2,0,1:T(4,128)}), f32[3,32,128]{2,0,1:T(4,128)S(1)}, u32[]{:S(2)}, u32[]{:S(2)}) %all-to-all-start.3) | async-done | bytes 49184 | tf_op jit(solution)/shard_map/all_to_all | solution.py:121
  511.8 0.9 broadcast_in_dim.8
  512.7 3.7 all-to-all-start.6
  516.4 17.8 %all-to-all-done.6 = f32[32,1,2049]{2,1,0:T(1,128)S(1)} async-done(((f32[32,1,2049]{2,1,0:T(1,128)}), f32[32,1,2049]{2,1,0:T(1,128)S(1)}, u32[]{:S(2)}, u32[]{:S(2)}) %all-to-all-start.6) | async-done | bytes 262304 | tf_op jit(solution)/shard_map/all_to_all | solution.py:37
  534.2 0.7 broadcast_in_dim.7
  534.8 9.3 %all-to-all-start.4 = ((f32[32,3,256]{2,1,0:T(4,128)}), f32[32,3,256]{2,1,0:T(4,128)S(1)}, u32[]{:S(2)}, u32[]{:S(2)}) async-start(f32[32,3,256]{2,1,0:T(4,128)} %broadcast_in_dim.7), calls=%async_computation.4 | async-start | bytes 262144 | tf_op jit(solution)/shard_map/all_to_all | solution.py:37
  544.2 0.7 reduce.5
  545.0 0.5 slice.25
  546.3 1.0 convolution_divide_fusion
  547.3 14.4 %all-to-all-done.4 = f32[32,3,256]{2,1,0:T(4,128)S(1)} async-done(((f32[32,3,256]{2,1,0:T(4,128)}), f32[32,3,256]{2,1,0:T(4,128)S(1)}, u32[]{:S(2)}, u32[]{:S(2)}) %all-to-all-start.4) | async-done | bytes 98336 | tf_op jit(solution)/shard_map/all_to_all | solution.py:37
  561.7 1.0 fusion.9
  (31 shorter events, 1.8 us)
Async XLA Ops:
  7.2 356.0 %copy-start = (bf16[384,256]{1,0:T(8,128)(2,1)S(1)}, bf16[384,256]{1,0:T(8,128)(2,1)}, u32[]{:S(2)}) copy-start(bf16[384,256]{1,0:T(8,128)(2,1)} %param.9) | copy-start | bytes 589828
  12.4 19.6 %copy-start.1 = (bf16[384,256]{1,0:T(8,128)(2,1)S(1)}, bf16[384,256]{1,0:T(8,128)(2,1)}, u32[]{:S(2)}) copy-start(bf16[384,256]{1,0:T(8,128)(2,1)} %param.10) | copy-start | bytes 589828
  12.4 402.4 %all-to-all-start = ((bf16[32,896,128]{1,2,0:T(8,128)(2,1)}), bf16[32,896,128]{1,2,0:T(8,128)(2,1)}, u32[]{:S(2)}, u32[]{:S(2)}) async-start(bf16[32,896,128]{1,2,0:T(8,128)(2,1)} %stack.2), calls=%async_computation | async-start | bytes 14680064 | tf_op jit(solution)/shard_map/all_to_all | solution.py:82
  31.9 331.2 %copy-start.2 = (bf16[256,64]{0,1:T(8,128)(2,1)S(1)}, bf16[256,64]{0,1:T(8,128)(2,1)}, u32[]{:S(2)}) copy-start(bf16[256,64]{0,1:T(8,128)(2,1)} %param.14) | copy-start | bytes 98308
  32.0 378.0 %all-gather.4.cloned.1.call-start = ((), (), s32[]{:S(2)}) async-start(), calls=%async_computation.7 | async-start | bytes 3932160 | tf_op jit(solution)/shard_map/all_gather | solution.py:19
  423.0 19.5 %copy-start.4 = (s32[3]{0:T(128)S(1)}, s32[3]{0:T(128)}, u32[]{:S(2)}) copy-start(s32[3]{0:T(128)} %param.16) | copy-start | bytes 40
  423.3 29.4 %copy-start.3 = (s32[16]{0:T(128)S(1)}, s32[16]{0:T(128)}, u32[]{:S(2)}) copy-start(s32[16]{0:T(128)} %param.17) | copy-start | bytes 196
  438.4 12.4 %all-to-all-start.2 = ((f32[16,1,3072]{2,1,0:T(1,128)}), f32[16,1,3072]{2,1,0:T(1,128)S(1)}, u32[]{:S(2)}, u32[]{:S(2)}) async-start(f32[16,1,3072]{2,1,0:T(1,128)} %broadcast_in_dim.6), calls=%async_computation.2 | async-start | bytes 393216 | tf_op jit(solution)/shard_map/all_to_all | solution.py:37
  454.9 35.2 %all-to-all-start.5 = ((f32[32,1,2049]{2,1,0:T(1,128)}), f32[32,1,2049]{2,1,0:T(1,128)S(1)}, u32[]{:S(2)}, u32[]{:S(2)}) async-start(f32[32,1,2049]{2,1,0:T(1,128)} %all_to_all.46), calls=%async_computation.5 | async-start | bytes 557056 | tf_op jit(solution)/shard_map/all_to_all | solution.py:54
  490.1 21.7 %all-to-all-start.3 = ((f32[3,32,128]{2,0,1:T(4,128)}), f32[3,32,128]{2,0,1:T(4,128)S(1)}, u32[]{:S(2)}, u32[]{:S(2)}) async-start(f32[3,32,128]{2,0,1:T(4,128)} %copy.54), calls=%async_computation.3 | async-start | bytes 131072 | tf_op jit(solution)/shard_map/all_to_all | solution.py:121
  512.7 21.5 %all-to-all-start.6 = ((f32[32,1,2049]{2,1,0:T(1,128)}), f32[32,1,2049]{2,1,0:T(1,128)S(1)}, u32[]{:S(2)}, u32[]{:S(2)}) async-start(f32[32,1,2049]{2,1,0:T(1,128)} %broadcast_in_dim.8), calls=%async_computation.6 | async-start | bytes 557056 | tf_op jit(solution)/shard_map/all_to_all | solution.py:37
  534.8 26.9 %all-to-all-start.4 = ((f32[32,3,256]{2,1,0:T(4,128)}), f32[32,3,256]{2,1,0:T(4,128)S(1)}, u32[]{:S(2)}, u32[]{:S(2)}) async-start(f32[32,3,256]{2,1,0:T(4,128)} %broadcast_in_dim.7), calls=%async_computation.4 | async-start | bytes 262144 | tf_op jit(solution)/shard_map/all_to_all | solution.py:37
Sparse Core Ops, SparseCore 0:
  363.3 46.6 all-gather.3
